TPU v7x, 32 devices: a whole 2x2x4 slice. The times are simulated.
32 devices in a mesh: groups: 2 (over y), adapter: 4 (over x, core), tensor: 4 (over z).
Axes of the slice: x: 2, y: 2, z: 4, core: 2. Of those that a mesh axis runs over, the one named last changes fastest.
Arguments:
- tokens: bfloat16 [2048, 8192], P(('groups', 'adapter'), 'tensor'), parts along dimension 0, may hold values from -6 to 6
- query_weight: bfloat16 [8192, 8192], P('tensor', 'adapter'), may hold values from -0.0625 to 0.0625
- adapter_down_weight: bfloat16 [128, 16, 8192], P('adapter', None, 'tensor'), may hold values from -0.0625 to 0.0625
- adapter_up_weight: bfloat16 [128, 16, 8192], P('adapter'), may hold values from -1.5 to 1.5
- block_adapter_ids: int32 [16], P('groups'), parts along dimension 0, may hold values from 0 to 127, as said below
- block_live_count: int32 [16], P('groups'), parts along dimension 0, may hold values from 1 to 128
- adapter_slot_index: int32 [256], P('groups'), parts along dimension 0, may hold values from 0 to 127, as said below
Outputs:
- query: bfloat16 [2048, 8192], P(('groups', 'tensor'), 'adapter'), parts along dimension 0
There are 2 independent parts, one for each index of `groups`. A program takes and returns all parts, laid end to end along the dimension named above; an argument that names none is the same for every part. Nothing has to cross between parts.
Inputs may be any that keep to these rules, and one draw needn't show every extreme that they name: Counting blocks by the owner range adapter_slot_index[block_adapter_ids[k]] // 32, no owner has more than 4 blocks, and one owner has exactly 4 in every draw. `adapter_slot_index`: A permutation: each slot holds exactly one adapter.
All inputs are finite; a program needn't handle non-finite values.
Results may differ from a plain program's by a relative error of at most 0.014.
Values may be sent and summed in bfloat16 or wider, within the bound.
A program may use at most 128 MiB of HBM per device.

v0:
```python
import jax
import jax.numpy as jnp
from jax import lax
from jax.sharding import PartitionSpec as P

BLOCK = 128


adapter_scale = 2.0


def block_plan(block_adapter_ids, adapter_slot_index, owners, adapters_per_device, capacity):
    adapters = adapter_slot_index.shape[0]
    picked = block_adapter_ids[:, None] == jnp.arange(adapters, dtype=jnp.int32)[None, :]
    block_slot_index = jnp.sum(jnp.where(picked, adapter_slot_index[None, :], 0), axis=1)
    owner_of = block_slot_index // adapters_per_device
    local_slot = block_slot_index % adapters_per_device
    hit_table = (owner_of[:, None] == jnp.arange(owners, dtype=jnp.int32)[None, :]).astype(
        jnp.int32
    )
    before = jnp.cumsum(hit_table, axis=0) - hit_table
    order_in = jnp.sum(before * hit_table, axis=1)
    return (owner_of, local_slot, order_in, owner_of * capacity + order_in)


def on_device(
    tokens,
    query_weight,
    adapter_down_weight,
    adapter_up_weight,
    block_adapter_ids,
    block_live_count,
    adapter_slot_index,
):
    owners = lax.axis_size("adapter")
    my_index = lax.axis_index("adapter")
    tok_dev = tokens.shape[0]
    features = tokens.shape[1]
    adapters_per_device = adapter_down_weight.shape[0]
    rank_width = adapter_down_weight.shape[1]
    blocks = block_adapter_ids.shape[0]
    blk_dev = blocks // owners
    capacity = 2 * blk_dev
    token_row_count = tok_dev * owners
    output_columns = query_weight.shape[1]
    owner_of, local_slot, order_in, packed = block_plan(
        block_adapter_ids, adapter_slot_index, owners, adapters_per_device, capacity
    )
    seat_ids = jnp.arange(capacity, dtype=jnp.int32)
    matches = (owner_of[None, :] == my_index) & (order_in[None, :] == seat_ids[:, None])
    filled = jnp.any(matches, axis=1)
    match_int = matches.astype(jnp.int32)
    block_ids = jnp.arange(blocks, dtype=jnp.int32)
    mine_block = jnp.sum(match_int * block_ids[None, :], axis=1)
    local_adapter_rows = jnp.sum(match_int * local_slot[None, :], axis=1)
    token_keep_mask = filled.astype(jnp.bfloat16)
    positions = jnp.arange(BLOCK, dtype=jnp.int32)
    up_weight_packed = (
        jnp.take(adapter_up_weight, local_adapter_rows, axis=0) * token_keep_mask[:, None, None]
    )
    up_recv = lax.all_to_all(up_weight_packed, "adapter", split_axis=2, concat_axis=0, tiled=True)
    down_mine = jnp.take(adapter_down_weight, local_adapter_rows, axis=0)
    mine_live = jnp.take(block_live_count, mine_block, axis=0)
    live_mine = ((positions[None, :] < mine_live[:, None]) & filled[:, None]).astype(jnp.float32)
    portion = lax.all_gather(tokens, "adapter", axis=0, tiled=True)
    piece_blocks = portion.shape[0] // BLOCK
    query_product = jnp.dot(portion, query_weight, preferred_element_type=jnp.float32)
    inside = ((mine_block >= 0) & (mine_block < piece_blocks)).astype(jnp.float32)
    chosen = jnp.take(
        portion.reshape(piece_blocks, BLOCK, features),
        jnp.clip(mine_block, 0, piece_blocks - 1),
        axis=0,
    )
    shrunk_piece = jnp.einsum("ksd,krd->ksr", chosen, down_mine, preferred_element_type=jnp.float32)
    shrunk_piece = shrunk_piece * (live_mine * inside[:, None])[:, :, None]
    shrunk_packs = lax.all_gather(shrunk_piece.astype(jnp.bfloat16), "adapter", axis=0, tiled=True)
    shrunk_all = jnp.take(shrunk_packs, packed, axis=0).reshape(token_row_count, rank_width)
    up_weight_blocks = jnp.take(up_recv, packed, axis=0)
    adapter_output = jnp.einsum(
        "ksr,krf->ksf",
        shrunk_all.reshape(blocks, BLOCK, rank_width),
        up_weight_blocks,
        preferred_element_type=jnp.float32,
    )
    partial_output = query_product + adapter_scale * adapter_output.reshape(
        token_row_count, output_columns
    )
    summed = lax.psum_scatter(
        partial_output.astype(jnp.bfloat16), "tensor", scatter_dimension=0, tiled=True
    )
    return summed


def solution(mesh):
    placed = (
        P(("groups", "adapter"), "tensor"),
        P("tensor", "adapter"),
        P("adapter", None, "tensor"),
        P("adapter", None, None),
        P("groups"),
        P("groups"),
        P("groups"),
    )
    return jax.shard_map(
        on_device,
        mesh=mesh,
        in_specs=placed,
        out_specs=P(("groups", "tensor"), "adapter"),
        check_vma=False,
    )
```

profile of v0, /device:TPU:17, one launch (start us, length us, event | category | flops | bytes accessed | tf_op | source)
XLA Modules:
  0.0 184.7 jit_solution(10934410185883613917)
XLA Ops:
  6.5 0.7 all-gather.2.cloned.1.call-update
  7.3 0.9 select_reduce_fusion
  8.1 0.2 reduce_window_sum.11
  8.3 0.1 fusion.30
  8.5 0.1 select_reduce_fusion.2
  8.7 5.0 %gather_fusion.4 = bf16[4,16,8192]{2,1,0:T(8,128)(2,1)} fusion(bf16[32,16,8192]{2,1,0:T(8,128)(2,1)} %param.10, s32[1024]{0:T(1024)S(1)} %pad_clamp_fusion.2), kind=kCustom, calls=%fused_computation.4 | custom fusion | bytes 2097168 | tf_op jit(solution)/shard_map/jit(_take)/gather | solution.py:59
  13.6 1.4 select_multiply_fusion
  15.0 8.2 %copy.14 = bf16[4,16,8192]{1,0,2:T(4,128)(2,1)} copy(bf16[4,16,8192]{2,1,0:T(8,128)(2,1)S(1)} %select_multiply_fusion) | data formatting | bytes 2097152 | tf_op jit(solution)/shard_map/mul | solution.py:59
  23.3 11.0 %reshape.291 = bf16[4,2,65536]{2,1,0:T(2,128)(2,1)} reshape(bf16[8192,4,16]{2,1,0:T(4,128)(2,1)} %bitcast.43) | data formatting | bytes 2097152
  34.3 4.1 %all-to-all-start = ((bf16[4,2,65536]{2,1,0:T(2,128)(2,1)}), bf16[4,2,65536]{2,1,0:T(2,128)(2,1)S(1)}, u32[]{:S(2)}, u32[]{:S(2)}) async-start(bf16[4,2,65536]{2,1,0:T(2,128)(2,1)} %reshape.291), calls=%async_computation | async-start | bytes 2097152 | tf_op jit(solution)/shard_map/all_to_all | solution.py:61
  38.4 0.6 gather_fusion.1
  39.0 0.6 gather_fusion.2
  39.8 14.4 %all-to-all-done = bf16[4,2,65536]{2,1,0:T(2,128)(2,1)S(1)} async-done(((bf16[4,2,65536]{2,1,0:T(2,128)(2,1)}), bf16[4,2,65536]{2,1,0:T(2,128)(2,1)S(1)}, u32[]{:S(2)}, u32[]{:S(2)}) %all-to-all-start) | async-done | bytes 1048608 | tf_op jit(solution)/shard_map/all_to_all | solution.py:61
  54.2 7.1 %reshape.292 = bf16[8192,4,16]{2,1,0:T(4,128)(2,1)} reshape(bf16[4,2,65536]{2,1,0:T(2,128)(2,1)S(1)} %all-to-all-done) | data formatting | bytes 2097152
  61.3 10.8 %copy.16 = bf16[4,4,16,2048]{3,2,1,0:T(8,128)(2,1)S(1)} copy(bf16[4,4,16,2048]{2,1,3,0:T(4,128)(2,1)} %bitcast.44) | data formatting | bytes 2097152 | tf_op jit(solution)/shard_map/all_to_all | solution.py:61
  72.1 1.4 gather_fusion.5
  73.5 4.3 %gather_fusion = bf16[4,128,2048]{2,1,0:T(8,128)(2,1)} fusion(bf16[8,128,2048]{2,1,0:T(8,128)(2,1)} %bitcast.46, s32[1024]{0:T(1024)S(1)} %pad_clamp_fusion.3), kind=kCustom, calls=%fused_computation | custom fusion | bytes 4194320 | tf_op jit(solution)/shard_map/jit(_take)/gather | solution.py:69
  77.7 2.3 %fusion.7 = bf16[4,128,16]{1,2,0:T(8,128)(2,1)S(1)} fusion(bf16[4,128,2048]{2,1,0:T(8,128)(2,1)} %gather_fusion, pred[4]{0:T(512)(128)(4,1)S(1)} %get-tuple-element.14, bf16[4,16,2048]{2,1,0:T(8,128)(2,1)S(1)} %gather_fusion.1, pred[4]{0:T(512)(128)(4,1)S(1)} %get-tuple-element.15, f32[4,128]{1,0:T(4,128)S(1)} %fusion.23), kind=kOutput, calls=%fused_computation.13 | convolution fusion | flops 34750464 | bytes 2377736 | tf_op jit(solution)/shard_map/ksd,krd->ksr/dot_general | solution.py:74
  80.1 5.6 %all_gather.7 = bf16[16,128,16]{1,2,0:T(8,128)(2,1)S(1)} all-gather(bf16[4,128,16]{1,2,0:T(8,128)(2,1)S(1)} %fusion.7), channel_id=1, replica_groups=mesh['groups'=2,'adapter'=4,'tensor'=4] {'adapter'}, dimensions={0}, use_global_device_ids=true | all-gather | bytes 81920 | tf_op jit(solution)/shard_map/all_gather | solution.py:76
  85.7 0.6 gather_fusion.3
  86.3 1.4 convolution_multiply_fusion
  87.6 0.8 copy-done.3
  88.4 12.5 %fusion = bf16[1024,2048]{1,0:T(8,128)(2,1)} fusion(f32[8,128,2048]{2,1,0:T(8,128)S(1)} %convolution_multiply_fusion, bf16[1024,2048]{1,0:T(8,128)(2,1)S(1)} %copy-done.3, bf16[2048,2048]{1,0:T(8,128)(2,1)} %param.8), kind=kOutput, calls=%fused_computation.7 | convolution fusion | flops 8594128896 | bytes 25165824 | tf_op jit(solution)/shard_map/dot_general | solution.py:67
  101.0 76.9 %reduce-scatter.2.cloned.1.call-done = bf16[256,2048]{1,0:T(8,128)(2,1)} async-done(((bf16[1024,2048]{1,0:T(8,128)(2,1)}), bf16[256,2048]{1,0:T(8,128)(2,1)}) %reduce-scatter.2.cloned.1.call-update) | async-done | bytes 1048592 | tf_op jit(solution)/shard_map/reduce_scatter | solution.py:88
  (26 shorter events, 0.2 us)
Async XLA Ops:
  6.5 31.9 %copy-start = (bf16[32,16,2048]{2,1,0:T(8,128)(2,1)S(1)}, bf16[32,16,2048]{2,1,0:T(8,128)(2,1)}, u32[]{:S(2)}) copy-start(bf16[32,16,2048]{2,1,0:T(8,128)(2,1)} %param.9) | copy-start | bytes 6291460
  6.5 66.9 %all-gather.2.cloned.1.call-start = ((), (), s32[]{:S(2)}) async-start(), calls=%async_computation.2 | async-start | bytes 5242880 | tf_op jit(solution)/shard_map/all_gather | solution.py:65
  23.3 15.7 %copy-start.1 = (s32[8]{0:T(128)S(1)}, s32[8]{0:T(128)}, u32[]{:S(2)}) copy-start(s32[8]{0:T(128)} %param.12) | copy-start | bytes 100
  34.3 19.9 %all-to-all-start = ((bf16[4,2,65536]{2,1,0:T(2,128)(2,1)}), bf16[4,2,65536]{2,1,0:T(2,128)(2,1)S(1)}, u32[]{:S(2)}, u32[]{:S(2)}) async-start(bf16[4,2,65536]{2,1,0:T(2,128)(2,1)} %reshape.291), calls=%async_computation | async-start | bytes 2097152 | tf_op jit(solution)/shard_map/all_to_all | solution.py:61
  38.4 139.5 %reduce-scatter.2.cloned.1.call-start = ((), (), s32[]{:S(2)}) async-start(), calls=%async_computation.3 | async-start | bytes 5242880 | tf_op jit(solution)/shard_map/reduce_scatter | solution.py:88
  73.5 12.8 %copy-start.2 = (bf16[8,16,2048]{2,1,0:T(8,128)(2,1)S(1)}, bf16[8,16,2048]{2,1,0:T(8,128)(2,1)}, u32[]{:S(2)}) copy-start(bf16[8,16,2048]{2,1,0:T(8,128)(2,1)} %gather_fusion.5) | copy-start | bytes 1572868
  86.2 2.2 %copy-start.3 = (bf16[1024,2048]{1,0:T(8,128)(2,1)S(1)}, bf16[1024,2048]{1,0:T(8,128)(2,1)}, u32[]{:S(2)}) copy-start(bf16[1024,2048]{1,0:T(8,128)(2,1)} %all-gather.2.cloned.1.call-done) | copy-start | bytes 12582916
Sparse Core Ops, SparseCore 0:
  8.9 37.8 all-gather.1
  101.1 76.7 reduce-scatter.1
where the time goes:
time: 186 us; the launch traced here: 185 us
  waiting for transfers between devices  92 us (49%)
  local copies, waits for them, and re-layouts  50.3 us (27%)
  matrix products  16.2 us (9%)
  between operations  13.5 us (7%)
  blocking collectives  5.62 us (3%)
  starting transfers between devices  4.13 us (2%)
  other arithmetic  2.9 us (2%)
    reduce_scatter x1, waiting for transfers between devices, on_device(): lax.psum_scatter(partial_output.astype(jnp.bfloat16), 'tensor', scatter_d...  76.9 us
    unnamed x10, local copies, waits for them, and re-layouts  18.9 us
    all_to_all x1, waiting for transfers between devices, on_device(): lax.all_to_all(up_weight_packed, 'adapter', split_axis=2, concat_axis=0,...  14.4 us
    dot_general x1, matrix products, on_device(): jnp.dot(portion, query_weight, preferred_element_type=jnp.float32)  12.5 us
    all_to_all x1, local copies, waits for them, and re-layouts, on_device(): lax.all_to_all(up_weight_packed, 'adapter', split_axis=2, concat_axis=0,...  10.8 us
    mul x1, local copies, waits for them, and re-layouts, on_device(): jnp.take(adapter_up_weight, local_adapter_rows, axis=0)  8.25 us
    all_gather x1, blocking collectives, on_device(): lax.all_gather(shrunk_piece.astype(jnp.bfloat16), 'adapter', axis=0, tile...  5.62 us
    gather x1, local copies, waits for them, and re-layouts, on_device(): jnp.take(adapter_up_weight, local_adapter_rows, axis=0)  4.97 us
  transfers between devices with their start and end apart: 3, of which 2 were waited for; matrix products, arithmetic and copies ran while one was open for 26% of the time, Pallas kernels for 0%

commit v1 on v0

v1 whole, which is shorter than its diff:
```python
import functools

import jax
import jax.numpy as jnp
from jax import lax
from jax.experimental import pallas as pl
from jax.experimental.pallas import tpu as pltpu
from jax.sharding import PartitionSpec as P

BLOCK = 128
SCALE = 2.0
MESH = pl.DeviceIdType.MESH


def kernel(
    A, T,
    ids, live, slots, tok_hbm, w_hbm, dn_hbm, up_hbm, out_ref,
    tok, w, dn, up, buf_r, buf_l, acc, dn_send, dn_recv, up_send, up_recv, s_send, s_recv,
    ld_sem, w_sem, tok_ss, tok_rs, dn_ss, dn_rs, up_ss, up_rs, s_ss, s_rs,
    r_ss, r_rs, l_ss, l_rs,
):
    a = lax.axis_index("adapter")
    t = lax.axis_index("tensor")
    chips = A // 2
    x, core = a // 2, a % 2
    partner = 2 * x + 1 - core
    rows_a = tok_hbm.shape[0]
    rows = rows_a * A
    rows_d = rows // T
    per_dev = dn_hbm.shape[0]
    np_, _, cp = buf_r.shape[1:]
    cols = np_ * cp
    nb_a = rows_a // BLOCK
    nb_t = rows_d // BLOCK

    def local(src, dst, i):
        return pltpu.make_async_copy(src, dst, ld_sem.at[i])

    my_rows = tok.at[pl.ds(pl.multiple_of(a * rows_a, rows_a), rows_a)]
    tok_load = local(tok_hbm, my_rows, 0)
    dn_load = local(dn_hbm, dn, 1)
    up_load = local(up_hbm, up, 2)
    tok_load.start()
    dn_load.start()

    def w_load(p):
        c = pl.ds(pl.multiple_of(p * cp, cp), cp)
        return pltpu.make_async_copy(w_hbm.at[:, c], w.at[p], w_sem.at[p])

    for p in range(np_):
        w_load(p).start()
    up_load.start()

    barrier = pltpu.get_barrier_semaphore()
    for i in range(1, A * T):
        q = (a * T + t + i) % (A * T)
        pl.semaphore_signal(
            barrier, inc=1, device_id={"adapter": q // T, "tensor": q % T}, device_id_type=MESH
        )
    pl.semaphore_wait(barrier, A * T - 1)

    def tok_copy(owner, to, ssem):
        r = tok.at[pl.ds(pl.multiple_of(owner * rows_a, rows_a), rows_a)]
        return pltpu.make_async_remote_copy(
            r, r, tok_ss.at[ssem], tok_rs.at[owner],
            device_id={"adapter": to}, device_id_type=MESH,
        )

    tok_load.wait()
    sends = [tok_copy(a, partner, 0)]
    for i in range(1, chips):
        sends.append(tok_copy(a, 2 * ((x + i) % chips) + core, i))
    for c in sends:
        c.start()

    def slot_of(k):
        return slots[ids[k]]

    dn_load.wait()
    for i in range(A):
        for b in range(nb_a):
            dn_send[i, b] = dn[lax.rem(slot_of(i * nb_a + b), per_dev)]
    dn_recv[a] = dn_send[a]

    def dn_copy(i):
        to = (a + i) % A
        return pltpu.make_async_remote_copy(
            dn_send.at[to], dn_recv.at[a], dn_ss.at[i], dn_rs.at[i],
            device_id={"adapter": to}, device_id_type=MESH,
        )

    for i in range(1, A):
        dn_copy(i).start()

    local_chunks = (2 * rows_a) // rows_d
    aligned = (2 * rows_a) % rows_d == 0 and local_chunks >= 2
    high = jnp.maximum((2 * (x + 1) * rows_a - 1) // rows_d, 1)
    low = jnp.minimum((2 * x * rows_a) // rows_d, T - 2)

    def order_r(j):
        v = T - j
        v = jnp.where(v <= high, v - 1, v)
        return jnp.where(j == 0, high, v)

    def order_l(j):
        v = j - 1
        v = jnp.where(v >= low, v + 1, v)
        return jnp.where(j == 0, low, v)

    pos_r = jnp.where(t == high, 0, jnp.where(t > high, T - t, T - 1 - t))
    pos_l = jnp.where(t == low, 0, jnp.where(t < low, t + 1, t))

    def base(d, p):
        return jnp.dot(
            tok[pl.ds(pl.multiple_of(d * rows_d, rows_d), rows_d), :], w[p],
            preferred_element_type=jnp.float32,
        )

    def flow(buf, ss, rs, to, j, p):
        return pltpu.make_async_remote_copy(
            buf.at[j, p], buf.at[j, p], ss.at[j, p], rs.at[j, p],
            device_id={"tensor": to}, device_id_type=MESH,
        )

    right, left = (t + 1) % T, (t + T - 1) % T

    def step(buf, ss, rs, to, d, j, p, fresh):
        @pl.when(fresh)
        def _():
            buf[j, p] = base(d, p).astype(buf.dtype)

        @pl.when(jnp.logical_not(fresh))
        def _():
            mine = base(d, p)
            flow(buf, ss, rs, to, j, p).wait_recv()
            buf[j, p] = (mine + buf[j, p].astype(jnp.float32)).astype(buf.dtype)

        flow(buf, ss, rs, to, j, p).start()

    def wait_tokens(first):
        for i in range(1, chips):
            o = 2 * ((x + i) % chips) + core
            tok_copy(o, partner, 0).wait_recv()
            tok_copy(o, partner, chips + i - 1).start()
        for i in range(1, chips):
            o = 2 * ((x + i) % chips) + 1 - core
            tok_copy(o, partner, 0).wait_recv()

    def up_copy(i):
        to = (a + i) % A
        return pltpu.make_async_remote_copy(
            up_send.at[to], up_recv.at[a], up_ss.at[i], up_rs.at[i],
            device_id={"adapter": to}, device_id_type=MESH,
        )

    def s_dest(b):
        k = a * nb_a + b
        return k // nb_t, k % nb_t

    def s_copy(i, b):
        d, kk = s_dest(b)
        return pltpu.make_async_remote_copy(
            s_send.at[b], s_recv.at[t, kk], s_ss.at[i, b], s_rs.at[t, kk],
            device_id={"adapter": (a + i) % A, "tensor": d}, device_id_type=MESH,
        )

    def send_adapters():
        up_load.wait()
        for b in range(nb_t):
            sl = lax.rem(slot_of(t * nb_t + b), per_dev)
            for i in range(A):
                up_send[i, b] = up[sl, :, i * cols:(i + 1) * cols]
        up_recv[a] = up_send[a]
        for i in range(1, A):
            up_copy(i).start()
        for i in range(1, A):
            dn_copy(i).wait_recv()
        for b in range(nb_a):
            k = a * nb_a + b
            mine = dn_recv[lax.div(slot_of(k), per_dev), b]
            rows_b = tok[pl.ds(pl.multiple_of(k * BLOCK, BLOCK), BLOCK), :]
            s = lax.dot_general(
                mine, rows_b, (((1,), (1,)), ((), ())), preferred_element_type=jnp.float32
            )
            keep = lax.broadcasted_iota(jnp.int32, s.shape, 1) < live[k]
            s_send[b] = jnp.where(keep, s, 0.0).astype(s_send.dtype)
            d, kk = s_dest(b)
            for i in range(A):
                if i:
                    s_copy(i, b).start()
                else:
                    @pl.when(d == t)
                    def _():
                        s_recv[t, kk] = s_send[b]

                    @pl.when(d != t)
                    def _():
                        s_copy(0, b).start()

    def wait_adapters():
        for i in range(1, A):
            up_copy(i).wait_recv()
        for b in range(nb_t):
            owner = (t * nb_t + b) // nb_a
            for tt in range(T):
                c = pltpu.make_async_remote_copy(
                    s_send.at[0], s_recv.at[tt, b], s_ss.at[0, 0], s_rs.at[tt, b],
                    device_id={"adapter": partner}, device_id_type=MESH,
                )

                @pl.when(jnp.logical_or(owner != a, t != tt))
                def _():
                    c.wait_recv()

    def add_adapters(p):
        for b in range(nb_t):
            own = lax.div(slot_of(t * nb_t + b), per_dev)
            u = up_recv[own, b, :, pl.ds(pl.multiple_of(p * cp, cp), cp)]
            lhs = s_recv[:, b].reshape(T * s_recv.shape[2], BLOCK)
            r = slice(b * BLOCK, (b + 1) * BLOCK)
            acc[p, r] = acc[p, r] + SCALE * lax.dot_general(
                lhs, jnp.concatenate([u] * T, axis=0), (((0,), (0,)), ((), ())),
                preferred_element_type=jnp.float32,
            )

    if not aligned:
        tok_copy(partner, partner, 0).wait_recv()
        wait_tokens(True)

    for j in range(T - 1):
        if j == 0 and aligned:
            tok_copy(partner, partner, 0).wait_recv()
        if j == min(1, T - 2):
            if aligned:
                wait_tokens(True)
            send_adapters()
        if j == T - 2:
            wait_adapters()
        d_r, d_l = order_r(j), order_l(j)

        def body(p, _):
            if j == 0:
                w_load(p).wait()

            @pl.when(d_r > t)
            def _():
                step(buf_r, r_ss, r_rs, right, d_r, j, p, t == 0)

            @pl.when(d_l < t)
            def _():
                step(buf_l, l_ss, l_rs, left, d_l, j, p, t == T - 1)

            if j == min(1, T - 2):
                acc[p] = base(t, p)
            if j == T - 2:
                add_adapters(p)
            return 0

        lax.fori_loop(0, np_, body, 0)

    def last(p, _):
        @pl.when(t > 0)
        def _():
            flow(buf_r, r_ss, r_rs, right, pos_r, p).wait_recv()
            acc[p] = acc[p] + buf_r[pos_r, p].astype(jnp.float32)

        @pl.when(t < T - 1)
        def _():
            flow(buf_l, l_ss, l_rs, left, pos_l, p).wait_recv()
            acc[p] = acc[p] + buf_l[pos_l, p].astype(jnp.float32)

        out_ref[:, pl.ds(pl.multiple_of(p * cp, cp), cp)] = acc[p].astype(out_ref.dtype)
        return 0

    lax.fori_loop(0, np_, last, 0)

    for c in sends:
        c.wait_send()
    for i in range(1, chips):
        tok_copy(a, partner, chips + i - 1).wait_send()
    for i in range(1, A):
        dn_copy(i).wait_send()
        up_copy(i).wait_send()
    for b in range(nb_a):
        d, _ = s_dest(b)
        for i in range(1, A):
            s_copy(i, b).wait_send()

        @pl.when(d != t)
        def _():
            s_copy(0, b).wait_send()
    for j in range(T - 1):
        d_r, d_l = order_r(j), order_l(j)

        def drain(p, _):
            @pl.when(d_r > t)
            def _():
                flow(buf_r, r_ss, r_rs, right, j, p).wait_send()

            @pl.when(d_l < t)
            def _():
                flow(buf_l, l_ss, l_rs, left, j, p).wait_send()
            return 0

        lax.fori_loop(0, np_, drain, 0)


def on_device(tokens, query_weight, down, up, ids, live, slots):
    A, T = lax.axis_size("adapter"), lax.axis_size("tensor")
    rows_a, feat = tokens.shape
    cols = query_weight.shape[1]
    rank = down.shape[1]
    rows_d = rows_a * A // T
    cp = min(256, cols)
    np_ = cols // cp
    nb_a, nb_t = rows_a // BLOCK, rows_d // BLOCK
    chips = A // 2
    bf, f32 = jnp.bfloat16, jnp.float32
    dma = pltpu.SemaphoreType.DMA
    smem = pl.BlockSpec(memory_space=pltpu.SMEM)
    hbm = pl.BlockSpec(memory_space=pl.ANY)
    return pl.pallas_call(
        functools.partial(kernel, A, T),
        out_shape=jax.ShapeDtypeStruct((rows_d, cols), bf),
        in_specs=[smem, smem, smem, hbm, hbm, hbm, hbm],
        out_specs=pl.BlockSpec(memory_space=pltpu.VMEM),
        scratch_shapes=[
            pltpu.VMEM((rows_a * A, feat), bf),
            pltpu.VMEM((np_, feat, cp), bf),
            pltpu.VMEM(down.shape, bf),
            pltpu.VMEM(up.shape, bf),
            pltpu.VMEM((T - 1, np_, rows_d, cp), bf),
            pltpu.VMEM((T - 1, np_, rows_d, cp), bf),
            pltpu.VMEM((np_, rows_d, cp), f32),
            pltpu.VMEM((A, nb_a, rank, feat), bf),
            pltpu.VMEM((A, nb_a, rank, feat), bf),
            pltpu.VMEM((A, nb_t, rank, cols), bf),
            pltpu.VMEM((A, nb_t, rank, cols), bf),
            pltpu.VMEM((nb_a, rank, BLOCK), bf),
            pltpu.VMEM((T, nb_t, rank, BLOCK), bf),
            dma((3,)), dma((np_,)),
            dma((2 * chips,)), dma((A,)),
            dma((A,)), dma((A,)), dma((A,)), dma((A,)),
            dma((A, nb_a)), dma((T, nb_t)),
            dma((T - 1, np_)), dma((T - 1, np_)), dma((T - 1, np_)), dma((T - 1, np_)),
        ],
        compiler_params=pltpu.CompilerParams(
            collective_id=0, has_side_effects=True, vmem_limit_bytes=60 * 1024 * 1024
        ),
    )(ids, live, slots, tokens, query_weight, down, up)


def solution(mesh):
    placed = (
        P(("groups", "adapter"), "tensor"),
        P("tensor", "adapter"),
        P("adapter", None, "tensor"),
        P("adapter", None, None),
        P("groups"),
        P("groups"),
        P("groups"),
    )
    return jax.shard_map(
        on_device,
        mesh=mesh,
        in_specs=placed,
        out_specs=P(("groups", "tensor"), "adapter"),
        check_vma=False,
    )
```

time: 186 us -> 93.6 us (0.50)
  waiting for transfers between devices: 92 us -> 0 us
  Pallas kernels: 0 us -> 91.1 us
  local copies, waits for them, and re-layouts: 50.3 us -> 2.3 us
  matrix products: 16.2 us -> 0 us
  between operations: 13.5 us -> 0.01 us
  blocking collectives: 5.62 us -> 0 us
  starting transfers between devices: 4.13 us -> 0 us
  other arithmetic: 2.9 us -> 0 us
    pallas_call x0 -> x1, Pallas kernels: none -> 91.1 us  [on_device(): pl.pallas_call(functools.partial(kernel, A, T), out_shape=jax.ShapeDtypeS...]
    reduce_scatter x1 -> x0, waiting for transfers between devices: 76.9 us -> none  [on_device(): lax.psum_scatter(partial_output.astype(jnp.bfloat16), 'tensor', scatter_d...]
    unnamed x10 -> x1, local copies, waits for them, and re-layouts: 18.9 us -> 2.3 us
    dot_general x3 -> x0, matrix products: 16.2 us -> none  [the longest x1 12.5 us: on_device(): jnp.dot(portion, query_weight, preferred_element_type=jnp.float32)]
    all_to_all x1 -> x0, waiting for transfers between devices: 14.4 us -> none  [on_device(): lax.all_to_all(up_weight_packed, 'adapter', split_axis=2, concat_axis=0,...]
    gather x6 -> x0, local copies, waits for them, and re-layouts: 12.4 us -> none  [the longest x1 4.97 us: on_device(): jnp.take(adapter_up_weight, local_adapter_rows, axis=0)]
    all_to_all x1 -> x0, local copies, waits for them, and re-layouts: 10.8 us -> none  [on_device(): lax.all_to_all(up_weight_packed, 'adapter', split_axis=2, concat_axis=0,...]
    mul x1 -> x0, local copies, waits for them, and re-layouts: 8.25 us -> none  [on_device(): jnp.take(adapter_up_weight, local_adapter_rows, axis=0)]
  transfers between devices with their start and end apart: 3 -> 0, of which waited for: 2 -> 0; matrix products, arithmetic and copies ran while one was open for 26% -> 0% of each run, Pallas kernels for 0% -> 0%
where the time goes in v1:
time: 93.6 us; the launch traced here: 93.4 us
  Pallas kernels  91.1 us (97%)
  local copies, waits for them, and re-layouts  2.3 us (2%)
    pallas_call x1, Pallas kernels, on_device(): pl.pallas_call(functools.partial(kernel, A, T), out_shape=jax.ShapeDtypeS...  91.1 us
    unnamed x1, local copies, waits for them, and re-layouts  2.3 us

profile of v1, /device:TPU:17, one launch (start us, length us, event | category | flops | bytes accessed | tf_op | source)
XLA Modules:
  0.0 93.4 jit_solution(14055967441889231968)
XLA Ops:
  0.0 91.1 %shard_map.73 = bf16[256,2048]{1,0:T(8,128)(2,1)} custom-call(s32[8]{0:T(128)} %ids.1, s32[8]{0:T(128)} %live.1, s32[128]{0:T(128)} %slots.1, bf16[256,2048]{1,0:T(8,128)(2,1)} %tok_hbm.1, bf16[2048,2048]{1,0:T(8,128)(2,1)} %w_hbm.1, bf16[32,16,2048]{2,1,0:T(8,128)(2,1)} %dn_hbm.1, bf16[32,16,8192]{2,1,0:T(8,128)(2,1)} %up_hbm.1), custom_call_target="tpu_custom_call" | custom-call | tf_op jit(solution)/shard_map/pallas_call | solution.py:322
  91.1 2.3 %copy.9 = bf16[256,2048]{1,0:T(8,128)(2,1)} copy(bf16[256,2048]{1,0:T(8,128)(2,1)} %shard_map.73) | data formatting | bytes 2097152

commit v2 on v1

--- a/solution.py
+++ b/solution.py
@@ -89,9 +89,6 @@
             device_id={"adapter": to}, device_id_type=MESH,
         )
 
-    for i in range(1, A):
-        dn_copy(i).start()
-
     local_chunks = (2 * rows_a) // rows_d
     aligned = (2 * rows_a) % rows_d == 0 and local_chunks >= 2
     high = jnp.maximum((2 * (x + 1) * rows_a - 1) // rows_d, 1)
@@ -173,6 +170,8 @@
         up_recv[a] = up_send[a]
         for i in range(1, A):
             up_copy(i).start()
+
+    def send_shrunk():
         for i in range(1, A):
             dn_copy(i).wait_recv()
         for b in range(nb_a):
@@ -233,9 +232,11 @@
         if j == min(1, T - 2):
             if aligned:
                 wait_tokens(True)
+            for i in range(1, A):
+                dn_copy(i).start()
             send_adapters()
         if j == T - 2:
-            wait_adapters()
+            send_shrunk()
         d_r, d_l = order_r(j), order_l(j)
 
         def body(p, _):
@@ -252,13 +253,15 @@
 
             if j == min(1, T - 2):
                 acc[p] = base(t, p)
-            if j == T - 2:
-                add_adapters(p)
             return 0
 
         lax.fori_loop(0, np_, body, 0)
 
+    wait_adapters()
+
     def last(p, _):
+        add_adapters(p)
+
         @pl.when(t > 0)
         def _():
             flow(buf_r, r_ss, r_rs, right, pos_r, p).wait_recv()

time: 93.6 us -> 92.5 us (0.988)
  Pallas kernels: 91.1 us -> 90 us
    pallas_call x1, Pallas kernels: 91.1 us -> 90 us  [on_device(): pl.pallas_call(functools.partial(kernel, A, T), out_shape=jax.ShapeDtypeS...]
where the time goes in v2:
time: 92.5 us; the launch traced here: 92.4 us
  Pallas kernels  90 us (97%)
  local copies, waits for them, and re-layouts  2.3 us (2%)
    pallas_call x1, Pallas kernels, on_device(): pl.pallas_call(functools.partial(kernel, A, T), out_shape=jax.ShapeDtypeS...  90 us
    unnamed x1, local copies, waits for them, and re-layouts  2.3 us

profile of v2, /device:TPU:17, one launch (start us, length us, event | category | flops | bytes accessed | tf_op | source)
XLA Modules:
  0.0 92.4 jit_solution(8148199423641758958)
XLA Ops:
  0.0 90.0 %shard_map.73 = bf16[256,2048]{1,0:T(8,128)(2,1)} custom-call(s32[8]{0:T(128)} %ids.1, s32[8]{0:T(128)} %live.1, s32[128]{0:T(128)} %slots.1, bf16[256,2048]{1,0:T(8,128)(2,1)} %tok_hbm.1, bf16[2048,2048]{1,0:T(8,128)(2,1)} %w_hbm.1, bf16[32,16,2048]{2,1,0:T(8,128)(2,1)} %dn_hbm.1, bf16[32,16,8192]{2,1,0:T(8,128)(2,1)} %up_hbm.1), custom_call_target="tpu_custom_call" | custom-call | tf_op jit(solution)/shard_map/pallas_call | solution.py:325
  90.1 2.3 %copy.9 = bf16[256,2048]{1,0:T(8,128)(2,1)} copy(bf16[256,2048]{1,0:T(8,128)(2,1)} %shard_map.73) | data formatting | bytes 2097152
